TPU v7x, 32 devices: a whole 2x2x4 slice. The times are simulated.
32 devices in a mesh: rows: 8 (over z, x), width: 4 (over y, core).
Axes of the slice: x: 2, y: 2, z: 4, core: 2. Of those that a mesh axis runs over, the one named last changes fastest.
Arguments:
- w_gate: float32 [3072, 8192], P('rows', 'width'), may hold values from -0.15625 to 0.15625
- avg_gate: float32 [3072, 8192], P('rows', 'width'), may hold values from -0.109375 to 0.109375
- w_up: float32 [3072, 8192], P('rows', 'width'), may hold values from -0.15625 to 0.15625
- avg_up: float32 [3072, 8192], P('rows', 'width'), may hold values from -0.109375 to 0.109375
- norm_gain: float32 [3072], P('rows'), may hold values from 0.25 to 1.75
Outputs:
- serve_gate: bfloat16 [3072, 8192], P(None, 'width')
- serve_up: bfloat16 [3072, 8192], P(None, 'width')
- factor_gate: float32 [8192], P('width')
- factor_up: float32 [8192], P('width')
All inputs are finite; a program needn't handle non-finite values. Where the computation divides by a largest or mean magnitude, that divisor is 1e-20 or more.
Results may differ from a plain program's by a relative error of at most 0.001.
Values may be sent and summed in bfloat16 or wider, within the bound.
A program may use at most 128 MiB of HBM per device.

v0:
```python
import jax
import jax.numpy as jnp
from jax import lax
from jax.sharding import PartitionSpec as P

keep_rate = 0.7


def local(w_gate, avg_gate, w_up, avg_up, norm_gain):
    fresh_gate = keep_rate * avg_gate + (1.0 - keep_rate) * w_gate
    fresh_up = keep_rate * avg_up + (1.0 - keep_rate) * w_up
    fresh_gained_gate = fresh_gate * norm_gain[:, None]
    fresh_gained_up = fresh_up * norm_gain[:, None]
    factor_gate, factor_up = lax.pmax(
        (jnp.max(jnp.abs(fresh_gained_gate), axis=0), jnp.max(jnp.abs(fresh_gained_up), axis=0)),
        "rows",
    )
    narrow_gate, narrow_up = (
        (fresh_gained_gate / factor_gate).astype(jnp.bfloat16),
        (fresh_gained_up / factor_up).astype(jnp.bfloat16),
    )
    serve_gate, serve_up = (
        lax.all_gather(narrow_gate, "rows", axis=0, tiled=True),
        lax.all_gather(narrow_up, "rows", axis=0, tiled=True),
    )
    return (serve_gate, serve_up, factor_gate, factor_up)


def solution(mesh):
    placed = (
        P("rows", "width"),
        P("rows", "width"),
        P("rows", "width"),
        P("rows", "width"),
        P("rows"),
    )
    return jax.shard_map(
        local,
        mesh=mesh,
        in_specs=placed,
        out_specs=(P(None, "width"), P(None, "width"), P("width"), P("width")),
        check_vma=False,
    )
```

profile of v0, /device:TPU:0, one launch (start us, length us, event | category | flops | bytes accessed | tf_op | source)
XLA Modules:
  0.0 432.8 jit_solution(5114650396990649841)
XLA Ops:
  7.2 0.0 copy-start.4
  7.2 0.0 copy-start.1
  7.2 0.0 all-gather.5.cloned.1.call-start
  7.2 5.8 %abs_reduce_fusion = (f32[2048]{0:T(1024)S(1)}, f32[2048]{0:T(1024)S(1)}) fusion(f32[384]{0:T(512)} %param.9, f32[384,2048]{1,0:T(8,128)} %param.7, f32[384,2048]{1,0:T(8,128)} %param.8, f32[384,2048]{1,0:T(8,128)} %param.5, f32[384,2048]{1,0:T(8,128)} %param.6), kind=kLoop, calls=%fused_computation.1 | loop fusion | flops 9433088 | bytes 12600832 | tf_op jit(solution)/shard_map/reduce_max | solution.py:15
  13.1 38.8 %all-reduce = (f32[2048]{0:T(1024)S(1)}, f32[2048]{0:T(1024)S(1)}) all-reduce(f32[2048]{0:T(1024)S(1)} %get-tuple-element.5, f32[2048]{0:T(1024)S(1)} %get-tuple-element.4), channel_id=1, replica_groups=mesh['rows'=8,'width'=4] {'rows'}, use_global_device_ids=true, to_apply=%region_1.0 | all-reduce | flops 4096 | bytes 32768 | tf_op jit(solution)/shard_map/pmax | solution.py:14
  51.9 0.0 copy-start.2
  51.9 0.0 copy-start.3
  51.9 0.0 copy-done.4
  51.9 0.0 copy-done.1
  51.9 5.7 %divide_convert_fusion = (bf16[384,2048]{1,0:T(8,128)(2,1)}, bf16[384,2048]{1,0:T(8,128)(2,1)}) fusion(f32[2048]{0:T(1024)S(1)} %get-tuple-element.17, f32[384]{0:T(512)S(1)} %copy-done.4, f32[384,2048]{1,0:T(8,128)S(1)} %copy-done.1, f32[384,2048]{1,0:T(8,128)} %param.8, f32[2048]{0:T(1024)S(1)} %get-tuple-element.16, f32[384,2048]{1,0:T(8,128)} %param.5, ...), kind=kLoop, calls=%fused_computation | loop fusion | flops 9437184 | bytes 15746560 | tf_op jit(solution)/shard_map/convert_element_type | solution.py:20
  57.7 0.0 copy-done.2
  57.7 0.0 copy-done.3
  57.7 0.0 all-gather.5.cloned.1.call-update
  57.7 0.0 all-gather.3.cloned.1.call-start
  57.8 0.7 all-gather.3.cloned.1.call-update
  58.5 172.8 %all-gather.5.cloned.1.call-done = bf16[3072,2048]{1,0:T(8,128)(2,1)} async-done(((bf16[384,2048]{1,0:T(8,128)(2,1)}), bf16[3072,2048]{1,0:T(8,128)(2,1)}) %all-gather.5.cloned.1.call-update) | async-done | bytes 12582928 | tf_op jit(solution)/shard_map/all_gather | solution.py:24
  231.2 177.1 %all-gather.3.cloned.1.call-done = bf16[3072,2048]{1,0:T(8,128)(2,1)} async-done(((bf16[384,2048]{1,0:T(8,128)(2,1)}), bf16[3072,2048]{1,0:T(8,128)(2,1)}) %all-gather.3.cloned.1.call-update) | async-done | bytes 12582928 | tf_op jit(solution)/shard_map/all_gather | solution.py:23
  408.3 0.0 copy-start
  408.3 11.4 %copy.11 = bf16[3072,2048]{1,0:T(8,128)(2,1)} copy(bf16[3072,2048]{1,0:T(8,128)(2,1)} %all-gather.3.cloned.1.call-done) | data formatting | bytes 25165824
  419.7 1.5 copy-done
  421.2 4.8 %copy.12 = bf16[3072,2048]{1,0:T(8,128)(2,1)} copy(bf16[3072,2048]{1,0:T(8,128)(2,1)S(1)} %copy-done) | data formatting | bytes 25165824
Async XLA Ops:
  7.2 44.8 %copy-start.4 = (f32[384]{0:T(512)S(1)}, f32[384]{0:T(512)}, u32[]{:S(2)}) copy-start(f32[384]{0:T(512)} %param.9) | copy-start | bytes 4612
  7.2 44.8 %copy-start.1 = (f32[384,2048]{1,0:T(8,128)S(1)}, f32[384,2048]{1,0:T(8,128)}, u32[]{:S(2)}) copy-start(f32[384,2048]{1,0:T(8,128)} %param.7) | copy-start | bytes 9437188
  7.2 224.1 %all-gather.5.cloned.1.call-start = ((), (), s32[]{:S(2)}) async-start(), calls=%async_computation.1 | async-start | bytes 14155776 | tf_op jit(solution)/shard_map/all_gather | solution.py:24
  51.9 5.8 %copy-start.2 = (f32[2048]{0:T(1024)}, f32[2048]{0:T(1024)S(1)}, u32[]{:S(2)}) copy-start(f32[2048]{0:T(1024)S(1)} %get-tuple-element.16) | copy-start | bytes 24580
  51.9 5.8 %copy-start.3 = (f32[2048]{0:T(1024)}, f32[2048]{0:T(1024)S(1)}, u32[]{:S(2)}) copy-start(f32[2048]{0:T(1024)S(1)} %get-tuple-element.17) | copy-start | bytes 24580
  57.7 350.6 %all-gather.3.cloned.1.call-start = ((), (), s32[]{:S(2)}) async-start(), calls=%async_computation | async-start | bytes 14155776 | tf_op jit(solution)/shard_map/all_gather | solution.py:23
  408.3 12.9 %copy-start = (bf16[3072,2048]{1,0:T(8,128)(2,1)S(1)}, bf16[3072,2048]{1,0:T(8,128)(2,1)}, u32[]{:S(2)}) copy-start(bf16[3072,2048]{1,0:T(8,128)(2,1)} %all-gather.5.cloned.1.call-done) | copy-start | bytes 37748740
Sparse Core Ops, SparseCore 0:
  57.8 173.3 all-gather.4
  234.0 174.2 all-gather.2
where the time goes:
time: 433 us
  waiting for transfers between devices  351 us (81%)
  blocking collectives  38.8 us (9%)
  local copies, waits for them, and re-layouts  17.7 us (4%)
  between operations  14.1 us (3%)
  other arithmetic  11.6 us (3%)
    all_gather x1, waiting for transfers between devices, local(): lax.all_gather(narrow_gate, 'rows', axis=0, tiled=True)  177 us
    all_gather x1, waiting for transfers between devices, local(): lax.all_gather(narrow_up, 'rows', axis=0, tiled=True)  173 us
    pmax x1, blocking collectives, local(): lax.pmax((jnp.max(jnp.abs(fresh_gained_gate), axis=0), jnp.max(jnp.abs(fr...  38.8 us
    unnamed x12, local copies, waits for them, and re-layouts  17.7 us
  transfers between devices with their start and end apart: 2, of which 2 were waited for; matrix products, arithmetic and copies ran while one was open for 0% of the time, Pallas kernels for 0%

commit v1 on v0

v1 whole, which is shorter than its diff:
```python
import functools

import jax
import jax.numpy as jnp
from jax import lax
from jax.experimental import pallas as pl
from jax.experimental.pallas import tpu as pltpu
from jax.sharding import PartitionSpec as P

keep_rate = 0.7
MESH = pl.DeviceIdType.MESH
CHUNKS = 4


def ring_place(r, n):
    if n % 2:
        return r
    x, z = r % 2, r // 2
    return z + x * (n - 1 - 2 * z)


def ring_row(p, n):
    if n % 2:
        return p
    half = n // 2
    x, k = p // half, p % half
    return 2 * (k + x * (half - 1 - 2 * k)) + x


def maxima_kernel(n, part_ref, out_ref, got, send_sem, recv_sem):
    me = lax.axis_index("rows")
    barrier = pltpu.get_barrier_semaphore()
    for d in range(1, n):
        pl.semaphore_signal(barrier, inc=1, device_id={"rows": (me + d) % n}, device_id_type=MESH)
    pl.semaphore_wait(barrier, n - 1)
    copies = []
    for d in range(1, n):
        copy = pltpu.make_async_remote_copy(
            src_ref=part_ref,
            dst_ref=got.at[d - 1],
            send_sem=send_sem.at[d - 1],
            recv_sem=recv_sem.at[d - 1],
            device_id={"rows": (me + d) % n},
            device_id_type=MESH,
        )
        copy.start()
        copies.append(copy)
    for copy in copies:
        copy.wait()
    out_ref[...] = jnp.maximum(part_ref[...], jnp.max(got[...], axis=0))


def maxima(part, n):
    return pl.pallas_call(
        functools.partial(maxima_kernel, n),
        out_shape=jax.ShapeDtypeStruct(part.shape, part.dtype),
        in_specs=[pl.BlockSpec(memory_space=pltpu.VMEM)],
        out_specs=pl.BlockSpec(memory_space=pltpu.VMEM),
        scratch_shapes=[
            pltpu.VMEM((n - 1,) + part.shape, part.dtype),
            pltpu.SemaphoreType.DMA((n - 1,)),
            pltpu.SemaphoreType.DMA((n - 1,)),
        ],
        compiler_params=pltpu.CompilerParams(collective_id=0, has_side_effects=True),
        name="maxima",
    )(part)


def ring_kernel(n, chunks, a_ref, b_ref, ao_ref, bo_ref, send_sem, recv_sem, own_sem):
    me = lax.axis_index("rows")
    place = ring_place(me, n)
    nxt = ring_row((place + 1) % n, n)
    prv = ring_row((place + n - 1) % n, n)
    rows = a_ref.shape[0]
    size = rows // chunks

    barrier = pltpu.get_barrier_semaphore()
    for other in (nxt, prv):
        pl.semaphore_signal(barrier, inc=1, device_id={"rows": other}, device_id_type=MESH)
    pl.semaphore_wait(barrier, 2)

    def here(owner, c):
        return pl.ds(pl.multiple_of(owner * rows + c * size, size), size)

    def send(way, step, c, first):
        src, out, to = ((a_ref, ao_ref, nxt), (b_ref, bo_ref, prv))[way]
        turn = (n - step) if way == 0 else step
        at = here(ring_row((place + turn) % n, n), c)
        return pltpu.make_async_remote_copy(
            src_ref=src.at[pl.ds(c * size, size)] if first else out.at[at],
            dst_ref=out.at[at],
            send_sem=send_sem.at[way, step, c],
            recv_sem=recv_sem.at[way, step, c],
            device_id={"rows": to},
            device_id_type=MESH,
        )

    for c in range(chunks):
        for way in range(2):
            send(way, 0, c, True).start()
    own = [
        pltpu.make_async_copy(src, out.at[pl.ds(pl.multiple_of(me * rows, rows), rows)], own_sem.at[way])
        for way, (src, out) in enumerate(((a_ref, ao_ref), (b_ref, bo_ref)))
    ]
    for copy in own:
        copy.start()

    def landed(way, step, c):
        src, out, to = ((a_ref, ao_ref, nxt), (b_ref, bo_ref, prv))[way]
        turn = (n - step - 1) if way == 0 else (step + 1)
        at = here(ring_row((place + turn) % n, n), c)
        pltpu.make_async_remote_copy(
            src_ref=out.at[at],
            dst_ref=out.at[at],
            send_sem=send_sem.at[way, step, c],
            recv_sem=recv_sem.at[way, step, c],
            device_id={"rows": to},
            device_id_type=MESH,
        ).wait_recv()

    @pl.loop(1, n - 1)
    def _(step):
        for c in range(chunks):
            for way in range(2):
                landed(way, step - 1, c)
                send(way, step, c, False).start()

    for c in range(chunks):
        for way in range(2):
            landed(way, n - 2, c)
    for copy in own:
        copy.wait()
    for c in range(chunks):
        for way in range(2):
            send(way, 0, c, True).wait_send()

    @pl.loop(1, n - 1)
    def _(step):
        for c in range(chunks):
            for way in range(2):
                send(way, step, c, False).wait_send()


def ring(a, b, n):
    rows, columns = a.shape
    chunks = CHUNKS
    while rows % (16 * chunks):
        chunks -= 1
    whole = jax.ShapeDtypeStruct((n * rows, columns), a.dtype)
    return pl.pallas_call(
        functools.partial(ring_kernel, n, chunks),
        out_shape=(whole, whole),
        in_specs=[pl.BlockSpec(memory_space=pltpu.VMEM)] * 2,
        out_specs=(pl.BlockSpec(memory_space=pl.ANY), pl.BlockSpec(memory_space=pl.ANY)),
        scratch_shapes=[
            pltpu.SemaphoreType.DMA((2, n - 1, chunks)),
            pltpu.SemaphoreType.DMA((2, n - 1, chunks)),
            pltpu.SemaphoreType.DMA((2,)),
        ],
        compiler_params=pltpu.CompilerParams(collective_id=1, has_side_effects=True),
        name="ring",
    )(a, b)


def local(n, w_gate, avg_gate, w_up, avg_up, norm_gain):
    gain = norm_gain[:, None]

    def fresh(avg, w):
        return (keep_rate * avg + (1.0 - keep_rate) * w) * gain

    part = jnp.stack([jnp.max(jnp.abs(fresh(avg, w)), axis=0) for avg, w in ((avg_gate, w_gate), (avg_up, w_up))])
    factor = maxima(part, n)
    narrow_gate = (fresh(avg_gate, w_gate) / factor[0]).astype(jnp.bfloat16)
    narrow_up = (fresh(avg_up, w_up) / factor[1]).astype(jnp.bfloat16)
    serve_gate, serve_up = ring(narrow_gate, narrow_up, n)
    return (serve_gate, serve_up, factor[0], factor[1])


def solution(mesh):
    placed = (P("rows", "width"),) * 4 + (P("rows"),)
    return jax.shard_map(
        functools.partial(local, mesh.shape["rows"]),
        mesh=mesh,
        in_specs=placed,
        out_specs=(P(None, "width"), P(None, "width"), P("width"), P("width")),
        check_vma=False,
    )
```

time: 433 us -> 284 us (0.66)
  waiting for transfers between devices: 351 us -> 0 us
  Pallas kernels: 0 us -> 253 us
  blocking collectives: 38.8 us -> 0 us
  between operations: 14.1 us -> 0.72 us
    all_gather x2 -> x0, waiting for transfers between devices: 350 us -> none  [the longest x1 177 us: local(): lax.all_gather(narrow_gate, 'rows', axis=0, tiled=True)]
    pallas_call x0 -> x2, Pallas kernels: none -> 253 us  [the longest x1 242 us: ring(): pl.pallas_call(functools.partial(ring_kernel, n, chunks), out_shape=(whol...]
    pmax x1 -> x0, blocking collectives: 38.8 us -> none  [local(): lax.pmax((jnp.max(jnp.abs(fresh_gained_gate), axis=0), jnp.max(jnp.abs(fr...]
  transfers between devices with their start and end apart: 2 -> 0, of which waited for: 2 -> 0; matrix products, arithmetic and copies ran while one was open for 0% -> 0% of each run, Pallas kernels for 0% -> 0%
where the time goes in v1:
time: 284 us
  Pallas kernels  253 us (89%)
  local copies, waits for them, and re-layouts  18.5 us (7%)
  other arithmetic  12.2 us (4%)
    pallas_call x1, Pallas kernels, ring(): pl.pallas_call(functools.partial(ring_kernel, n, chunks), out_shape=(whol...  242 us
    unnamed x12, local copies, waits for them, and re-layouts  17.7 us
    pallas_call x1, Pallas kernels, maxima(): pl.pallas_call(functools.partial(maxima_kernel, n), out_shape=jax.ShapeDt...  10.6 us
    reduce_max x1, other arithmetic, local(): jnp.max(jnp.abs(fresh(avg, w)), axis=0)  5.85 us
    convert_element_type x1, other arithmetic, local(): narrow_up = (fresh(avg_up, w_up) / factor[1]).astype(jnp.bfloat16)  5.75 us

profile of v1, /device:TPU:0, one launch (start us, length us, event | category | flops | bytes accessed | tf_op | source)
XLA Modules:
  0.0 284.0 jit_solution(4218938006610696201)
XLA Ops:
  0.6 0.0 copy-start.4
  0.6 0.0 copy-start.1
  0.7 5.8 %abs_reduce_fusion.1 = (f32[2048]{0:T(1024)S(1)}, f32[2048]{0:T(1024)S(1)}) fusion(f32[384]{0:T(512)} %param.9, f32[384,2048]{1,0:T(8,128)} %param.5, f32[384,2048]{1,0:T(8,128)} %param.6, f32[384,2048]{1,0:T(8,128)} %param.7, f32[384,2048]{1,0:T(8,128)} %param.8), kind=kLoop, calls=%fused_computation.4 | loop fusion | flops 9433088 | bytes 12600832 | tf_op jit(solution)/shard_map/reduce_max | solution.py:171
  6.5 0.6 pad_maximum_fusion.part_ref
  7.1 10.6 %maxima.1 = f32[2,2048]{1,0:T(2,128)} custom-call(f32[2,2048]{1,0:T(2,128)} %pad_maximum_fusion.part_ref), custom_call_target="tpu_custom_call" | custom-call | tf_op jit(solution)/shard_map/maxima/pallas_call | solution.py:54
  17.8 0.8 fusion
  18.6 0.0 copy-start.2
  18.6 0.0 copy-start.3
  18.6 0.0 copy-done.4
  18.6 0.0 copy-done.1
  18.6 5.7 %divide_convert_fusion = (bf16[384,2048]{1,0:T(8,128)(2,1)}, bf16[384,2048]{1,0:T(8,128)(2,1)}) fusion(f32[2048]{0:T(1024)S(1)} %bitcast.4, f32[384]{0:T(512)S(1)} %copy-done.4, f32[384,2048]{1,0:T(8,128)} %param.7, f32[384,2048]{1,0:T(8,128)} %param.8, f32[2048]{0:T(1024)S(1)} %bitcast.6, f32[384,2048]{1,0:T(8,128)S(1)} %copy-done.1, f32[384,2048]{1,0:T(8,128)} %param.6), kind=kLoop, calls=%fused_computation | loop fusion | flops 9437184 | bytes 15746560 | tf_op jit(solution)/shard_map/convert_element_type | solution.py:174
  24.4 0.0 copy-done.2
  24.4 0.0 copy-done.3
  24.4 242.0 %ring.1 = (bf16[3072,2048]{1,0:T(8,128)(2,1)}, bf16[3072,2048]{1,0:T(8,128)(2,1)}) custom-call(bf16[384,2048]{1,0:T(8,128)(2,1)} %get-tuple-element.13.a_ref, bf16[384,2048]{1,0:T(8,128)(2,1)} %get-tuple-element.12.b_ref), custom_call_target="tpu_custom_call" | custom-call | tf_op jit(solution)/shard_map/ring/pallas_call | solution.py:150
  266.3 0.0 copy-start
  266.3 11.4 %copy.11 = bf16[3072,2048]{1,0:T(8,128)(2,1)} copy(bf16[3072,2048]{1,0:T(8,128)(2,1)} %get-tuple-element.18) | data formatting | bytes 25165824
  277.7 1.5 copy-done
  279.2 4.8 %copy.12 = bf16[3072,2048]{1,0:T(8,128)(2,1)} copy(bf16[3072,2048]{1,0:T(8,128)(2,1)S(1)} %copy-done) | data formatting | bytes 25165824
Async XLA Ops:
  0.6 18.0 %copy-start.4 = (f32[384]{0:T(512)S(1)}, f32[384]{0:T(512)}, u32[]{:S(2)}) copy-start(f32[384]{0:T(512)} %param.9) | copy-start | bytes 4612
  0.6 18.0 %copy-start.1 = (f32[384,2048]{1,0:T(8,128)S(1)}, f32[384,2048]{1,0:T(8,128)}, u32[]{:S(2)}) copy-start(f32[384,2048]{1,0:T(8,128)} %param.5) | copy-start | bytes 9437188
  18.6 5.8 %copy-start.2 = (f32[1,2048]{1,0:T(1,128)}, f32[1,2048]{1,0:T(1,128)S(1)}, u32[]{:S(2)}) copy-start(f32[1,2048]{1,0:T(1,128)S(1)} %get-tuple-element.10) | copy-start | bytes 24580
  18.6 5.8 %copy-start.3 = (f32[1,2048]{1,0:T(1,128)}, f32[1,2048]{1,0:T(1,128)S(1)}, u32[]{:S(2)}) copy-start(f32[1,2048]{1,0:T(1,128)S(1)} %get-tuple-element.11) | copy-start | bytes 24580
  266.3 12.9 %copy-start = (bf16[3072,2048]{1,0:T(8,128)(2,1)S(1)}, bf16[3072,2048]{1,0:T(8,128)(2,1)}, u32[]{:S(2)}) copy-start(bf16[3072,2048]{1,0:T(8,128)(2,1)} %get-tuple-element.19) | copy-start | bytes 37748740

commit v2 on v1

v2 whole, which is shorter than its diff:
```python
import functools

import jax
import jax.numpy as jnp
from jax import lax
from jax.experimental import pallas as pl
from jax.experimental.pallas import tpu as pltpu
from jax.sharding import PartitionSpec as P

keep_rate = 0.7
MESH = pl.DeviceIdType.MESH
CHUNKS = 4
VMEM_LIMIT = 60 * 2**20


def ring_place(r, n):
    if n % 2:
        return r
    x, z = r % 2, r // 2
    return z + x * (n - 1 - 2 * z)


def ring_row(p, n):
    if n % 2:
        return p
    half = n // 2
    x, k = p // half, p % half
    return 2 * (k + x * (half - 1 - 2 * k)) + x


def serve_kernel(
    n, chunks, gain_ref, wg_ref, ag_ref, wu_ref, au_ref, go_ref, uo_ref, fg_ref, fu_ref,
    w_in, fresh, narrow, part, got, in_sem, max_send, max_recv, send_sem, recv_sem, own_sem,
):
    me = lax.axis_index("rows")
    place = ring_place(me, n)
    nxt = ring_row((place + 1) % n, n)
    prv = ring_row((place + n - 1) % n, n)
    rows, columns = wg_ref.shape
    size = rows // chunks
    outs, to = (go_ref, uo_ref), (nxt, prv)

    loads = []
    for c in range(chunks):
        at = pl.ds(c * size, size)
        for k, (w_ref, avg_ref) in enumerate(((wg_ref, ag_ref), (wu_ref, au_ref))):
            for j, (src, dst) in enumerate(((w_ref, w_in), (avg_ref, fresh))):
                load = pltpu.make_async_copy(src.at[at], dst.at[k, at], in_sem.at[c, k, j])
                load.start()
                loads.append(load)

    barrier = pltpu.get_barrier_semaphore()
    for d in range(1, n):
        pl.semaphore_signal(barrier, inc=1, device_id={"rows": (me + d) % n}, device_id_type=MESH)

    tops = [jnp.zeros((8, columns), jnp.float32)] * 2
    for c in range(chunks):
        for k in range(2):
            loads[(c * 2 + k) * 2].wait()
            loads[(c * 2 + k) * 2 + 1].wait()

            def blend(i, top):
                at = pl.ds(pl.multiple_of(c * size + i * 8, 8), 8)
                gain = jnp.tile(gain_ref[at, :], (1, columns // 128))
                value = (keep_rate * fresh[k, at, :] + (1.0 - keep_rate) * w_in[k, at, :]) * gain
                fresh[k, at, :] = value
                return jnp.maximum(top, jnp.abs(value))

            tops[k] = lax.fori_loop(0, size // 8, blend, tops[k])
    for k in range(2):
        part[k : k + 1, :] = jnp.max(tops[k], axis=0, keepdims=True)

    pl.semaphore_wait(barrier, n - 1)
    copies = []
    for d in range(1, n):
        copy = pltpu.make_async_remote_copy(
            src_ref=part,
            dst_ref=got.at[d - 1],
            send_sem=max_send.at[d - 1],
            recv_sem=max_recv.at[d - 1],
            device_id={"rows": (me + d) % n},
            device_id_type=MESH,
        )
        copy.start()
        copies.append(copy)
    for copy in copies:
        copy.wait()
    factor = jnp.maximum(part[...], jnp.max(got[...], axis=0))
    fg_ref[...] = factor[0:1]
    fu_ref[...] = factor[1:2]
    scale = 1.0 / factor

    def here(turn, c):
        owner = ring_row((place + turn) % n, n)
        return pl.ds(pl.multiple_of(owner * rows + c * size, size), size)

    def send(way, step, c, first=False):
        at = here((n - step) if way == 0 else step, c)
        return pltpu.make_async_remote_copy(
            src_ref=narrow.at[way, pl.ds(c * size, size)] if first else outs[way].at[at],
            dst_ref=outs[way].at[at],
            send_sem=send_sem.at[way, step, c],
            recv_sem=recv_sem.at[way, step, c],
            device_id={"rows": to[way]},
            device_id_type=MESH,
        )

    def landed(way, step, c):
        at = here((n - step - 1) if way == 0 else (step + 1), c)
        pltpu.make_async_remote_copy(
            src_ref=outs[way].at[at],
            dst_ref=outs[way].at[at],
            send_sem=send_sem.at[way, step, c],
            recv_sem=recv_sem.at[way, step, c],
            device_id={"rows": to[way]},
            device_id_type=MESH,
        ).wait_recv()

    for c in range(chunks + 1):
        for way in range(2):
            if c < chunks:
                by = jnp.broadcast_to(scale[way : way + 1, :], (16, columns))

                @pl.loop(0, size // 16)
                def _(i):
                    at = pl.ds(pl.multiple_of(c * size + i * 16, 16), 16)
                    narrow[way, at, :] = (fresh[way, at, :] * by).astype(jnp.bfloat16)

            if c:
                send(way, 0, c - 1, True).start()
    own = [
        pltpu.make_async_copy(
            narrow.at[way], outs[way].at[pl.ds(pl.multiple_of(me * rows, rows), rows)], own_sem.at[way]
        )
        for way in range(2)
    ]
    for copy in own:
        copy.start()

    @pl.loop(1, n - 1)
    def _(step):
        for c in range(chunks):
            for way in range(2):
                landed(way, step - 1, c)
                send(way, step, c).start()

    for c in range(chunks):
        for way in range(2):
            landed(way, n - 2, c)

    for copy in own:
        copy.wait()
    for c in range(chunks):
        for way in range(2):
            send(way, 0, c, True).wait_send()

    @pl.loop(1, n - 1)
    def _(step):
        for c in range(chunks):
            for way in range(2):
                send(way, step, c).wait_send()


def serve(w_gate, avg_gate, w_up, avg_up, norm_gain, n):
    rows, columns = w_gate.shape
    chunks = CHUNKS
    while rows % (16 * chunks):
        chunks -= 1
    whole = jax.ShapeDtypeStruct((n * rows, columns), jnp.bfloat16)
    line = jax.ShapeDtypeStruct((1, columns), jnp.float32)
    gain = jnp.broadcast_to(norm_gain[:, None], (rows, 128))
    anywhere = pl.BlockSpec(memory_space=pl.ANY)
    near = pl.BlockSpec(memory_space=pltpu.VMEM)
    return pl.pallas_call(
        functools.partial(serve_kernel, n, chunks),
        out_shape=(whole, whole, line, line),
        in_specs=[near] + [anywhere] * 4,
        out_specs=(anywhere, anywhere, near, near),
        scratch_shapes=[
            pltpu.VMEM((2, rows, columns), jnp.float32),
            pltpu.VMEM((2, rows, columns), jnp.float32),
            pltpu.VMEM((2, rows, columns), jnp.bfloat16),
            pltpu.VMEM((2, columns), jnp.float32),
            pltpu.VMEM((n - 1, 2, columns), jnp.float32),
            pltpu.SemaphoreType.DMA((chunks, 2, 2)),
            pltpu.SemaphoreType.DMA((n - 1,)),
            pltpu.SemaphoreType.DMA((n - 1,)),
            pltpu.SemaphoreType.DMA((2, n - 1, chunks)),
            pltpu.SemaphoreType.DMA((2, n - 1, chunks)),
            pltpu.SemaphoreType.DMA((2,)),
        ],
        compiler_params=pltpu.CompilerParams(
            collective_id=0, has_side_effects=True, vmem_limit_bytes=VMEM_LIMIT
        ),
        name="serve",
    )(gain, w_gate, avg_gate, w_up, avg_up)


def local(n, w_gate, avg_gate, w_up, avg_up, norm_gain):
    serve_gate, serve_up, factor_gate, factor_up = serve(w_gate, avg_gate, w_up, avg_up, norm_gain, n)
    return (serve_gate, serve_up, factor_gate[0], factor_up[0])


def solution(mesh):
    placed = (P("rows", "width"),) * 4 + (P("rows"),)
    return jax.shard_map(
        functools.partial(local, mesh.shape["rows"]),
        mesh=mesh,
        in_specs=placed,
        out_specs=(P(None, "width"), P(None, "width"), P("width"), P("width")),
        check_vma=False,
    )
```

time: 284 us -> 274 us (0.965)
  other arithmetic: 12.2 us -> 0 us
    reduce_max x1 -> x0, other arithmetic: 5.85 us -> none  [local(): jnp.max(jnp.abs(fresh(avg, w)), axis=0)]
    convert_element_type x1 -> x0, other arithmetic: 5.75 us -> none  [local(): narrow_up = (fresh(avg_up, w_up) / factor[1]).astype(jnp.bfloat16)]
    unnamed x12 -> x10, local copies, waits for them, and re-layouts: 17.7 us -> 18.9 us
    pallas_call x2 -> x1, Pallas kernels: 253 us -> 253 us  [serve(): pl.pallas_call(functools.partial(serve_kernel, n, chunks), out_shape=(who...]
where the time goes in v2:
time: 274 us
  Pallas kernels  253 us (92%)
  local copies, waits for them, and re-layouts  20.4 us (7%)
    pallas_call x1, Pallas kernels, serve(): pl.pallas_call(functools.partial(serve_kernel, n, chunks), out_shape=(who...  253 us
    unnamed x10, local copies, waits for them, and re-layouts  18.9 us

profile of v2, /device:TPU:0, one launch (start us, length us, event | category | flops | bytes accessed | tf_op | source)
XLA Modules:
  0.0 273.7 jit_solution(10289897247105381226)
XLA Ops:
  0.6 1.5 broadcast_in_dim.2.gain_ref
  2.1 252.7 %serve.1 = (bf16[3072,2048]{1,0:T(8,128)(2,1)}, bf16[3072,2048]{1,0:T(8,128)(2,1)}, f32[1,2048]{1,0:T(1,128)}, f32[1,2048]{1,0:T(1,128)}) custom-call(f32[384,128]{1,0:T(8,128)} %broadcast_in_dim.2.gain_ref, f32[384,2048]{1,0:T(8,128)} %wg_ref.1, f32[384,2048]{1,0:T(8,128)} %ag_ref.1, f32[384,2048]{1,0:T(8,128)} %wu_ref.1, f32[384,2048]{1,0:T(8,128)} %au_ref.1), custom_call_target="tpu_custom_call" | custom-call | tf_op jit(solution)/shard_map/serve/pallas_call | solution.py:174
  254.9 0.0 copy-start
  254.9 11.4 %copy.13 = bf16[3072,2048]{1,0:T(8,128)(2,1)} copy(bf16[3072,2048]{1,0:T(8,128)(2,1)} %get-tuple-element.16) | data formatting | bytes 25165824
  266.2 1.5 copy-done
  267.8 0.0 copy-start.2
  267.8 0.0 copy-start.1
  267.8 4.8 %copy.14 = bf16[3072,2048]{1,0:T(8,128)(2,1)} copy(bf16[3072,2048]{1,0:T(8,128)(2,1)S(1)} %copy-done) | data formatting | bytes 25165824
  272.5 0.0 copy-done.2
  272.5 0.6 copy.15
  273.1 0.0 copy-done.1
  273.1 0.6 copy.16
Async XLA Ops:
  254.9 12.9 %copy-start = (bf16[3072,2048]{1,0:T(8,128)(2,1)S(1)}, bf16[3072,2048]{1,0:T(8,128)(2,1)}, u32[]{:S(2)}) copy-start(bf16[3072,2048]{1,0:T(8,128)(2,1)} %get-tuple-element.17) | copy-start | bytes 37748740
  267.8 4.8 %copy-start.2 = (f32[1,2048]{1,0:T(1,128)S(1)}, f32[1,2048]{1,0:T(1,128)}, u32[]{:S(2)}) copy-start(f32[1,2048]{1,0:T(1,128)} %get-tuple-element.10) | copy-start | bytes 24580
  267.8 5.4 %copy-start.1 = (f32[1,2048]{1,0:T(1,128)S(1)}, f32[1,2048]{1,0:T(1,128)}, u32[]{:S(2)}) copy-start(f32[1,2048]{1,0:T(1,128)} %get-tuple-element.11) | copy-start | bytes 24580

commit v3 on v2

--- a/solution.py
+++ b/solution.py
@@ -30,7 +30,7 @@
 
 def serve_kernel(
     n, chunks, gain_ref, wg_ref, ag_ref, wu_ref, au_ref, go_ref, uo_ref, fg_ref, fu_ref,
-    w_in, fresh, narrow, part, got, in_sem, max_send, max_recv, send_sem, recv_sem, own_sem,
+    w_in, fresh, narrow, gains, part, got, in_sem, max_send, max_recv, send_sem, recv_sem, own_sem,
 ):
     me = lax.axis_index("rows")
     place = ring_place(me, n)
@@ -53,6 +53,11 @@
     for d in range(1, n):
         pl.semaphore_signal(barrier, inc=1, device_id={"rows": (me + d) % n}, device_id_type=MESH)
 
+    for first in range(0, rows, 128):
+        count = min(128, rows - first)
+        line = gain_ref[first : first + count].reshape(1, count)
+        gains[first : first + count, :] = jnp.broadcast_to(line, (128, count)).T
+
     tops = [jnp.zeros((8, columns), jnp.float32)] * 2
     for c in range(chunks):
         for k in range(2):
@@ -61,7 +66,7 @@
 
             def blend(i, top):
                 at = pl.ds(pl.multiple_of(c * size + i * 8, 8), 8)
-                gain = jnp.tile(gain_ref[at, :], (1, columns // 128))
+                gain = jnp.tile(gains[at, :], (1, columns // 128))
                 value = (keep_rate * fresh[k, at, :] + (1.0 - keep_rate) * w_in[k, at, :]) * gain
                 fresh[k, at, :] = value
                 return jnp.maximum(top, jnp.abs(value))
@@ -168,7 +173,6 @@
         chunks -= 1
     whole = jax.ShapeDtypeStruct((n * rows, columns), jnp.bfloat16)
     line = jax.ShapeDtypeStruct((1, columns), jnp.float32)
-    gain = jnp.broadcast_to(norm_gain[:, None], (rows, 128))
     anywhere = pl.BlockSpec(memory_space=pl.ANY)
     near = pl.BlockSpec(memory_space=pltpu.VMEM)
     return pl.pallas_call(
@@ -180,6 +184,7 @@
             pltpu.VMEM((2, rows, columns), jnp.float32),
             pltpu.VMEM((2, rows, columns), jnp.float32),
             pltpu.VMEM((2, rows, columns), jnp.bfloat16),
+            pltpu.VMEM((rows, 128), jnp.float32),
             pltpu.VMEM((2, columns), jnp.float32),
             pltpu.VMEM((n - 1, 2, columns), jnp.float32),
             pltpu.SemaphoreType.DMA((chunks, 2, 2)),
@@ -193,7 +198,7 @@
             collective_id=0, has_side_effects=True, vmem_limit_bytes=VMEM_LIMIT
         ),
         name="serve",
-    )(gain, w_gate, avg_gate, w_up, avg_up)
+    )(norm_gain, w_gate, avg_gate, w_up, avg_up)
 
 
 def local(n, w_gate, avg_gate, w_up, avg_up, norm_gain):

time: 274 us -> 272 us (level)
  no operation moved by 1% of the time
where the time goes in v3:
time: 272 us
  Pallas kernels  253 us (93%)
  local copies, waits for them, and re-layouts  18.9 us (7%)
    pallas_call x1, Pallas kernels, serve(): pl.pallas_call(functools.partial(serve_kernel, n, chunks), out_shape=(who...  253 us
    unnamed x10, local copies, waits for them, and re-layouts  18.9 us

profile of v3, /device:TPU:0, one launch (start us, length us, event | category | flops | bytes accessed | tf_op | source)
XLA Modules:
  0.0 272.0 jit_solution(16039847958899854879)
XLA Ops:
  0.6 252.5 %serve.1 = (bf16[3072,2048]{1,0:T(8,128)(2,1)}, bf16[3072,2048]{1,0:T(8,128)(2,1)}, f32[1,2048]{1,0:T(1,128)}, f32[1,2048]{1,0:T(1,128)}) custom-call(f32[384]{0:T(512)} %gain_ref.1, f32[384,2048]{1,0:T(8,128)} %wg_ref.1, f32[384,2048]{1,0:T(8,128)} %ag_ref.1, f32[384,2048]{1,0:T(8,128)} %wu_ref.1, f32[384,2048]{1,0:T(8,128)} %au_ref.1), custom_call_target="tpu_custom_call" | custom-call | tf_op jit(solution)/shard_map/serve/pallas_call | solution.py:178
  253.2 0.0 copy-start
  253.2 11.4 %copy.13 = bf16[3072,2048]{1,0:T(8,128)(2,1)} copy(bf16[3072,2048]{1,0:T(8,128)(2,1)} %get-tuple-element.16) | data formatting | bytes 25165824
  264.5 1.5 copy-done
  266.1 0.0 copy-start.2
  266.1 0.0 copy-start.1
  266.1 4.8 %copy.14 = bf16[3072,2048]{1,0:T(8,128)(2,1)} copy(bf16[3072,2048]{1,0:T(8,128)(2,1)S(1)} %copy-done) | data formatting | bytes 25165824
  270.8 0.0 copy-done.2
  270.8 0.6 copy.15
  271.4 0.0 copy-done.1
  271.4 0.6 copy.16
Async XLA Ops:
  253.2 12.9 %copy-start = (bf16[3072,2048]{1,0:T(8,128)(2,1)S(1)}, bf16[3072,2048]{1,0:T(8,128)(2,1)}, u32[]{:S(2)}) copy-start(bf16[3072,2048]{1,0:T(8,128)(2,1)} %get-tuple-element.17) | copy-start | bytes 37748740
  266.1 4.8 %copy-start.2 = (f32[1,2048]{1,0:T(1,128)S(1)}, f32[1,2048]{1,0:T(1,128)}, u32[]{:S(2)}) copy-start(f32[1,2048]{1,0:T(1,128)} %get-tuple-element.10) | copy-start | bytes 24580
  266.1 5.4 %copy-start.1 = (f32[1,2048]{1,0:T(1,128)S(1)}, f32[1,2048]{1,0:T(1,128)}, u32[]{:S(2)}) copy-start(f32[1,2048]{1,0:T(1,128)} %get-tuple-element.11) | copy-start | bytes 24580
